TPU v7x, 32 devices: a whole 2x2x4 slice. The times are simulated.
32 devices in a mesh: ep: 8 (over z, x), tp: 4 (over y, core).
Axes of the slice: x: 2, y: 2, z: 4, core: 2. Of those that a mesh axis runs over, the one named last changes fastest.
Arguments:
- tokens: bfloat16 [2048, 2048], P('ep', 'tp'), may hold values from -180 to 180
- norm_gain: float32 [2048], replicated, may hold values from 0.1 to 1.9
- router_weight: bfloat16 [2048, 60], P('tp'), may hold values from -2 to 2
- shared_gate_w: bfloat16 [2048], replicated, may hold values from -0.125 to 0.125
- expert_ids: int32 [2048, 4], P('ep'), may hold values from 0 to 59, all different within a row; in each aligned block of 256 rows (0 to 255, 256 to 511, ...) at most 32 rows name the same one
- w_gate: bfloat16 [64, 2048, 1408], P('ep', None, 'tp'), may hold values from -0.125 to 0.125
- w_up: bfloat16 [64, 2048, 1408], P('ep', None, 'tp'), may hold values from -0.125 to 0.125
- w_down: bfloat16 [64, 1408, 2048], P('ep', 'tp'), may hold values from -1.5 to 1.5
- shared_w_gate: bfloat16 [2048, 2816], P(None, 'tp'), may hold values from -0.125 to 0.125
- shared_w_up: bfloat16 [2048, 2816], P(None, 'tp'), may hold values from -0.125 to 0.125
- shared_w_down: bfloat16 [2816, 2048], P('tp'), may hold values from -0.109375 to 0.109375
Outputs:
- moe_out: bfloat16 [2048, 2048], P('ep', 'tp')
Inputs may be any that keep to these rules, and one draw needn't show every extreme that they name: `expert_ids`: each row names 4 different experts below 60. Within the 256 rows of one index of ep no expert is named by more than 32 rows, and in some of these blocks one expert is named by exactly 32 rows.
All inputs are finite; a program needn't handle non-finite values.
Results may differ from a plain program's by a relative error of at most 0.0069.
Values may be sent and summed in bfloat16 or wider, within the bound.
A program may use at most 128 MiB of HBM per device.

v0:
```python
import jax
import jax.numpy as jnp
from jax import lax
from jax.sharding import PartitionSpec as P


def send_back(summed):
    return lax.all_to_all(summed, "ep", split_axis=0, concat_axis=0, tiled=True)


def expert_rows(arrived, w_gate, w_up, w_down):
    gate_act = jnp.einsum("sekd,edf->sekf", arrived, w_gate, preferred_element_type=jnp.float32)
    up_act = jnp.einsum("sekd,edf->sekf", arrived, w_up, preferred_element_type=jnp.float32)
    hidden = (jax.nn.silu(gate_act) * up_act).astype(jnp.bfloat16)
    partial_out = jnp.einsum("sekf,efd->sekd", hidden, w_down, preferred_element_type=jnp.float32)
    summed = lax.psum_scatter(partial_out, "tp", scatter_dimension=3, tiled=True).astype(
        jnp.bfloat16
    )
    return send_back(summed)


def sliced_rows(arrived, w_gate, w_up, w_down):
    complete = lax.all_gather(arrived, "tp", axis=3, tiled=True)
    return expert_rows(complete, w_gate, w_up, w_down)


def per_device(
    tokens,
    norm_gain,
    router_weight,
    shared_gate_w,
    expert_ids,
    w_gate,
    w_up,
    w_down,
    shared_w_gate,
    shared_w_up,
    shared_w_down,
):
    width = tokens.shape[1]
    tok_rows = tokens.shape[0]
    column_start = lax.axis_index("tp") * width
    whole = lax.all_gather(tokens, "tp", axis=1, tiled=True)
    values = whole.astype(jnp.float32)
    inv_rms = lax.rsqrt(jnp.mean(values * values, axis=-1, keepdims=True) + 1e-06)
    normed = (values * inv_rms * norm_gain[None, :]).astype(jnp.bfloat16)
    own_part = lax.dynamic_slice_in_dim(normed, column_start, width, 1)
    partial_logits = jnp.dot(own_part, router_weight, preferred_element_type=jnp.float32)
    logits = lax.psum(partial_logits, "tp")
    probs = jax.nn.softmax(logits, axis=-1)
    expert_count = logits.shape[1]
    matches = expert_ids[:, :, None] == jnp.arange(expert_count, dtype=jnp.int32)[None, None, :]
    route_weight = jnp.sum(jnp.where(matches, probs[:, None, :], 0.0), axis=-1)
    gate_whole, up_whole, down_whole = (w_gate, w_up, w_down)
    experts_here = w_gate.shape[0]
    slot_count = lax.axis_size("ep") * experts_here
    capacity = tok_rows // 8
    flat_ids = expert_ids.reshape(-1)
    one_hot = (flat_ids[:, None] == jnp.arange(slot_count, dtype=jnp.int32)[None, :]).astype(
        jnp.int32
    )
    before = jnp.cumsum(one_hot, axis=0) - one_hot
    order_rank = jnp.sum(before * one_hot, axis=1)
    slot_ids = (flat_ids * capacity + order_rank).reshape(expert_ids.shape)
    targets = jnp.arange(slot_count * capacity, dtype=jnp.int32)
    dispatch_map = jnp.sum(
        (slot_ids[None, :, :] == targets[:, None, None]).astype(jnp.bfloat16), axis=2
    )
    outgoing = jnp.dot(dispatch_map, own_part, preferred_element_type=jnp.float32).astype(
        jnp.bfloat16
    )
    outgoing = outgoing.reshape(lax.axis_size("ep"), experts_here, capacity, width)
    returned = sliced_rows(
        lax.all_to_all(outgoing, "ep", split_axis=0, concat_axis=0, tiled=True),
        w_gate=gate_whole,
        w_up=up_whole,
        w_down=down_whole,
    )
    picked = returned.reshape(slot_count * capacity, width)[slot_ids]
    routed = jnp.sum(route_weight[:, :, None] * picked.astype(jnp.float32), axis=1)
    shared_gate_act = jnp.dot(normed, shared_w_gate, preferred_element_type=jnp.float32)
    shared_up_act = jnp.dot(normed, shared_w_up, preferred_element_type=jnp.float32)
    shared_hidden = (jax.nn.silu(shared_gate_act) * shared_up_act).astype(jnp.bfloat16)
    shared_part = jnp.dot(shared_hidden, shared_w_down, preferred_element_type=jnp.float32)
    shared_own = lax.psum_scatter(shared_part, "tp", scatter_dimension=1, tiled=True)
    share_gate = jax.nn.sigmoid(jnp.dot(normed, shared_gate_w, preferred_element_type=jnp.float32))
    return (share_gate[:, None] * shared_own + routed).astype(jnp.bfloat16)


def solution(mesh):
    return jax.shard_map(
        per_device,
        mesh=mesh,
        in_specs=(
            P("ep", "tp"),
            P(),
            P("tp", None),
            P(),
            P("ep", None),
            P("ep", None, "tp"),
            P("ep", None, "tp"),
            P("ep", "tp", None),
            P(None, "tp"),
            P(None, "tp"),
            P("tp", None),
        ),
        out_specs=P("ep", "tp"),
        check_vma=False,
    )
```

profile of v0, /device:TPU:0, one launch (start us, length us, event | category | flops | bytes accessed | tf_op | source)
XLA Modules:
  0.0 386.9 jit_solution(7075725763673382850)
XLA Ops:
  6.5 0.7 all-gather.3.cloned.1.call-update
  7.3 0.9 copy.47
  8.5 18.0 %reduce-window.6 = s32[64,8,128]{2,1,0:T(8,128)S(1)} reduce-window(s32[64,8,128]{2,1,0:T(8,128)S(1)} %fusion.31, s32[]{:T(128)} %constant.8.clone.1), window={size=1x1x128 pad=0_0x0_0x127_0}, to_apply=%region_6.7 | reduce-window | flops 8323072 | bytes 524292 | tf_op jit(solution)/shard_map/reduce-window
  26.7 0.1 copy.49
  26.9 0.1 broadcast_add_fusion
  27.4 2.5 fusion.10
  29.9 1.6 fusion.15
  31.5 1.5 fusion.17
  33.1 0.7 convolution_convert_fusion
  33.8 0.2 copy-done.1
  34.0 55.3 %all_to_all.10 = bf16[8,8,32,512]{3,2,1,0:T(8,128)(2,1)S(1)} all-to-all(bf16[8,8,32,512]{3,2,1,0:T(8,128)(2,1)S(1)} %bitcast.87), channel_id=1, replica_groups=mesh['ep'=8,'tp'=4] {'ep'}, dimensions={0} | all-to-all | bytes 4194304 | tf_op jit(solution)/shard_map/all_to_all | solution.py:74
  89.3 1.6 copy.52
  91.0 57.4 %all-gather.5.cloned.1.call-done = bf16[8,8,32,2048]{3,2,0,1:T(8,128)(2,1)} async-done(((bf16[8,8,32,512]{3,2,0,1:T(8,128)(2,1)}), bf16[8,8,32,2048]{3,2,0,1:T(8,128)(2,1)}) %all-gather.5.cloned.1.call-update) | async-done | bytes 8388624 | tf_op jit(solution)/shard_map/all_gather | solution.py:23
  148.4 12.9 %fusion.4 = f32[8,8,32,352]{3,2,1,0:T(8,128)} fusion(bf16[8,8,32,2048]{3,2,0,1:T(8,128)(2,1)} %all-gather.5.cloned.1.call-done, bf16[8,2048,352]{1,2,0:T(8,128)(2,1)} %param.16), kind=kOutput, calls=%fused_computation.5 | convolution fusion | flops 2952790016 | bytes 22806528 | tf_op jit(solution)/shard_map/sekd,edf->sekf/dot_general | solution.py:12
  161.3 21.7 %fusion.7 = f32[8,8,32,2048]{3,2,0,1:T(8,128)} fusion(bf16[8,352,2048]{2,1,0:T(8,128)(2,1)} %param.18, f32[8,8,32,352]{3,2,1,0:T(8,128)} %fusion.4, bf16[8,8,32,2048]{3,2,0,1:T(8,128)(2,1)} %all-gather.5.cloned.1.call-done, bf16[8,2048,352]{1,2,0:T(8,128)(2,1)} %param.17), kind=kOutput, calls=%fused_computation.9 | convolution fusion | flops 5909905408 | bytes 51118080 | tf_op jit(solution)/shard_map/sekf,efd->sekd/dot_general | solution.py:15
  183.0 0.2 reduce-scatter.3.cloned.1.call-start
  183.2 4.0 %fusion.41 = f32[256,704]{0,1:T(8,128)} fusion(bf16[256,2048]{1,0:T(8,128)(2,1)} %copy-done.1, bf16[2048,704]{0,1:T(8,128)(2,1)} %param.19), kind=kOutput, calls=%fused_computation.60 | convolution fusion | flops 738197504 | bytes 4653056 | tf_op jit(solution)/shard_map/dot_general | solution.py:81
  187.2 7.6 %fusion.21 = f32[256,2048]{1,0:T(8,128)} fusion(bf16[704,2048]{1,0:T(8,128)(2,1)S(1)} %copy-done, bf16[256,2048]{1,0:T(8,128)(2,1)} %copy-done.1, bf16[2048,704]{0,1:T(8,128)(2,1)} %param.20, f32[256,704]{0,1:T(8,128)} %fusion.41), kind=kOutput, calls=%fused_computation.27 | convolution fusion | flops 1477476352 | bytes 9633792 | tf_op jit(solution)/shard_map/dot_general | solution.py:84
  194.8 113.2 %reduce-scatter.5.cloned.1.call-done = f32[8,8,32,512]{3,2,0,1:T(8,128)} async-done(((f32[8,8,32,2048]{3,2,0,1:T(8,128)}), f32[8,8,32,512]{3,2,0,1:T(8,128)}) %reduce-scatter.5.cloned.1.call-update) | async-done | bytes 4194320 | tf_op jit(solution)/shard_map/reduce_scatter | solution.py:16
  308.0 2.5 convert_element_type.44
  310.6 1.4 copy.53
  312.0 5.6 %all-to-all-start.1 = ((bf16[8,8,32,512]{3,2,1,0:T(8,128)(2,1)}), bf16[8,8,32,512]{3,2,1,0:T(8,128)(2,1)}, u32[]{:S(2)}, u32[]{:S(2)}) async-start(bf16[8,8,32,512]{3,2,1,0:T(8,128)(2,1)} %copy.53), calls=%async_computation.3 | async-start | bytes 4194304 | tf_op jit(solution)/shard_map/all_to_all | solution.py:8
  317.7 0.1 copy.54
  318.0 1.2 fusion.33
  319.1 11.7 %psum.7 = f32[256,60]{0,1:T(8,128)S(1)} all-reduce(f32[256,60]{0,1:T(8,128)S(1)} %fusion.33), channel_id=1, replica_groups=mesh['ep'=8,'tp'=4] {'tp'}, use_global_device_ids=true, to_apply=%region_2.0 | all-reduce | flops 15360 | bytes 122880 | tf_op jit(solution)/shard_map/psum | solution.py:49
  331.1 0.1 copy.46
  331.2 1.6 fusion.40
  332.8 33.0 %all-to-all-done.1 = bf16[8,8,32,512]{3,2,1,0:T(8,128)(2,1)} async-done(((bf16[8,8,32,512]{3,2,1,0:T(8,128)(2,1)}), bf16[8,8,32,512]{3,2,1,0:T(8,128)(2,1)}, u32[]{:S(2)}, u32[]{:S(2)}) %all-to-all-start.1) | async-done | bytes 2097184 | tf_op jit(solution)/shard_map/all_to_all | solution.py:8
  365.8 7.0 %gather_fusion = bf16[1024,512]{1,0:T(8,128)(2,1)} fusion(bf16[2048,512]{1,0:T(8,128)(2,1)} %bitcast.13, s32[1024]{0:T(1024)S(1)} %broadcast_clamp_fusion), kind=kCustom, calls=%fused_computation | custom fusion | bytes 2101248 | tf_op jit(solution)/shard_map/gather | solution.py:79
  372.8 2.8 reshape.60
  375.5 2.9 multiply_reduce_fusion
  378.5 1.9 add_convert_fusion
  (41 shorter events, 1.3 us)
Async XLA Ops:
  6.5 180.7 %copy-start = (bf16[704,2048]{1,0:T(8,128)(2,1)S(1)}, bf16[704,2048]{1,0:T(8,128)(2,1)}, u32[]{:S(2)}) copy-start(bf16[704,2048]{1,0:T(8,128)(2,1)} %param.21) | copy-start | bytes 8650756
  6.5 20.8 %copy-start.4 = (s32[256,4]{0,1:T(4,128)S(1)}, s32[256,4]{0,1:T(4,128)}, u32[]{:S(2)}) copy-start(s32[256,4]{0,1:T(4,128)} %param.15) | copy-start | bytes 12292
  6.5 25.0 %copy-start.5 = (f32[2048]{0:T(1024)S(1)}, f32[2048]{0:T(1024)}, u32[]{:S(2)}) copy-start(f32[2048]{0:T(1024)} %param.12) | copy-start | bytes 24580
  6.5 23.4 %all-gather.3.cloned.1.call-start = ((), (), s32[]{:S(2)}) async-start(), calls=%async_computation.4 | async-start | bytes 1310720 | tf_op jit(solution)/shard_map/all_gather | solution.py:43
  7.3 141.2 %all-gather.5.cloned.1.call-start = ((), (), s32[]{:S(2)}) async-start(), calls=%async_computation.6 | async-start | bytes 10485760 | tf_op jit(solution)/shard_map/all_gather | solution.py:23
  29.9 3.2 copy-start.2
  33.1 1.0 copy-start.1
  91.0 217.1 %reduce-scatter.5.cloned.1.call-start = ((), (), s32[]{:S(2)}) async-start(), calls=%async_computation.7 | async-start | bytes 20971520 | tf_op jit(solution)/shard_map/reduce_scatter | solution.py:16
  183.0 195.5 %reduce-scatter.3.cloned.1.call-start = ((), (), s32[]{:S(2)}) async-start(), calls=%async_computation.5 | async-start | bytes 2621440 | tf_op jit(solution)/shard_map/reduce_scatter | solution.py:85
  312.0 5.6 %copy-start.6 = (bf16[2048]{0:T(1024)(128)(2,1)S(1)}, bf16[2048]{0:T(1024)(128)(2,1)}, u32[]{:S(2)}) copy-start(bf16[2048]{0:T(1024)(128)(2,1)} %param.14) | copy-start | bytes 12292
  312.0 5.9 %copy-start.3 = (bf16[512,60]{0,1:T(8,128)(2,1)S(1)}, bf16[512,60]{0,1:T(8,128)(2,1)}, u32[]{:S(2)}) copy-start(bf16[512,60]{0,1:T(8,128)(2,1)} %param.13) | copy-start | bytes 184324
  312.0 53.8 %all-to-all-start.1 = ((bf16[8,8,32,512]{3,2,1,0:T(8,128)(2,1)}), bf16[8,8,32,512]{3,2,1,0:T(8,128)(2,1)}, u32[]{:S(2)}, u32[]{:S(2)}) async-start(bf16[8,8,32,512]{3,2,1,0:T(8,128)(2,1)} %copy.53), calls=%async_computation.3 | async-start | bytes 4194304 | tf_op jit(solution)/shard_map/all_to_all | solution.py:8
Sparse Core Ops, SparseCore 0:
  8.9 19.4 all-gather.2
  91.1 57.2 all-gather.4
  183.1 124.8 reduce-scatter.4
  310.4 31.3 reduce-scatter.2
where the time goes:
time: 388 us; the launch traced here: 387 us
  waiting for transfers between devices  204 us (53%)
  blocking collectives  67 us (17%)
  matrix products  49.6 us (13%)
  other arithmetic  31.4 us (8%)
  local copies, waits for them, and re-layouts  15.1 us (4%)
  between operations  13.4 us (3%)
  starting transfers between devices  5.95 us (2%)
    reduce_scatter x1, waiting for transfers between devices, expert_rows(): lax.psum_scatter(partial_out, 'tp', scatter_dimension=3, tiled=True)  113 us
    all_gather x1, waiting for transfers between devices, sliced_rows(): complete = lax.all_gather(arrived, 'tp', axis=3, tiled=True)  57.4 us
    all_to_all x1, blocking collectives, per_device(): lax.all_to_all(outgoing, 'ep', split_axis=0, concat_axis=0, tiled=True)  55.3 us
    all_to_all x1, waiting for transfers between devices, send_back(): return lax.all_to_all(summed, 'ep', split_axis=0, concat_axis=0, tiled=True)  33 us
    dot_general x1, matrix products, expert_rows(): jnp.einsum('sekf,efd->sekd', hidden, w_down, preferred_element_type=jnp.f...  21.7 us
    another operation x3, other arithmetic  18.2 us
    dot_general x1, matrix products, expert_rows(): jnp.einsum('sekd,edf->sekf', arrived, w_gate, preferred_element_type=jnp....  12.9 us
    psum x1, blocking collectives, per_device(): logits = lax.psum(partial_logits, 'tp')  11.7 us
  transfers between devices with their start and end apart: 5, of which 3 were waited for; matrix products, arithmetic and copies ran while one was open for 14% of the time, Pallas kernels for 0%

commit v1 on v0

--- a/solution.py
+++ b/solution.py
@@ -2,6 +2,9 @@
 import jax.numpy as jnp
 from jax import lax
 from jax.sharding import PartitionSpec as P
+
+F32 = jnp.float32
+BF16 = jnp.bfloat16
 
 
 def send_back(summed):
@@ -24,7 +27,7 @@
     return expert_rows(complete, w_gate, w_up, w_down)
 
 
-def per_device(
+def dispatch_plan(
     tokens,
     norm_gain,
     router_weight,
@@ -87,7 +90,79 @@
     return (share_gate[:, None] * shared_own + routed).astype(jnp.bfloat16)
 
 
+def gather_plan(
+    tokens,
+    norm_gain,
+    router_weight,
+    shared_gate_w,
+    expert_ids,
+    w_gate,
+    w_up,
+    w_down,
+    shared_w_gate,
+    shared_w_up,
+    shared_w_down,
+):
+    rows, width = tokens.shape
+    n_ep = lax.axis_size("ep")
+    n_tp = lax.axis_size("tp")
+    full = n_tp * width
+    here = w_gate.shape[0]
+    cap = rows // 8
+    me = lax.axis_index("ep")
+
+    every = lax.all_gather(tokens, ("ep", "tp"), axis=0)
+    ids = lax.all_gather(expert_ids, "ep", axis=0)
+    router = lax.all_gather(router_weight, "tp", axis=0, tiled=True)
+
+    whole = every.reshape(n_ep, n_tp, rows, width).transpose(0, 2, 1, 3)
+    values = whole.reshape(n_ep, rows, full).astype(F32)
+    inv_rms = lax.rsqrt(jnp.mean(values * values, axis=-1, keepdims=True) + 1e-06)
+    normed = (values * inv_rms * norm_gain).astype(BF16)
+
+    logits = jnp.einsum("std,dx->stx", normed, router, preferred_element_type=F32)
+    probs = jax.nn.softmax(logits, axis=-1)
+    probs = jnp.pad(probs, ((0, 0), (0, 0), (0, n_ep * here - probs.shape[-1])))
+    local = lax.dynamic_slice_in_dim(probs, me * here, here, 2)
+    names = me * here + jnp.arange(here, dtype=jnp.int32)
+    match = jnp.any(ids[:, :, :, None] == names, axis=2)
+    lower = jnp.tril(jnp.ones((rows, rows), BF16), -1)
+    rank = jnp.einsum("tu,suj->sjt", lower, match.astype(BF16), preferred_element_type=F32)
+    match_t = match.transpose(0, 2, 1)
+    spot = jnp.where(match_t, rank, -1.0).astype(jnp.int32)
+    pick = spot[:, :, None, :] == jnp.arange(cap, dtype=jnp.int32)[None, None, :, None]
+    slot_w = jnp.sum(jnp.where(pick, local.transpose(0, 2, 1)[:, :, None, :], 0.0), axis=-1)
+    pick = pick.astype(BF16)
+
+    x = jnp.einsum("sjkt,std->jskd", pick, normed, preferred_element_type=F32).astype(BF16)
+    gate = jnp.einsum("jskd,jdf->jskf", x, w_gate, preferred_element_type=F32)
+    up = jnp.einsum("jskd,jdf->jskf", x, w_up, preferred_element_type=F32)
+    hidden = (jax.nn.silu(gate) * up).astype(BF16)
+    y = jnp.einsum("jskf,jfd->jskd", hidden, w_down, preferred_element_type=F32)
+    y = (y * slot_w.transpose(1, 0, 2)[..., None]).astype(BF16)
+    routed = jnp.einsum("sjkt,jskd->std", pick, y, preferred_element_type=F32)
+
+    own = lax.dynamic_index_in_dim(normed, me, 0, keepdims=False)
+    sg = jnp.dot(own, shared_w_gate, preferred_element_type=F32)
+    su = jnp.dot(own, shared_w_up, preferred_element_type=F32)
+    sh = (jax.nn.silu(sg) * su).astype(BF16)
+    part = jnp.dot(sh, shared_w_down, preferred_element_type=F32)
+    share = jax.nn.sigmoid(jnp.dot(own, shared_gate_w, preferred_element_type=F32))
+    part = share[:, None] * part
+    mine = (jnp.arange(n_ep) == me)[:, None, None]
+    total = (routed + jnp.where(mine, part[None], 0.0)).astype(BF16)
+    total = total.reshape(n_ep, rows, n_tp, width)
+    total = lax.psum_scatter(total, "tp", scatter_dimension=2, tiled=True)
+    total = total.reshape(n_ep * rows, width)
+    return lax.psum_scatter(total, "ep", scatter_dimension=0, tiled=True)
+
+
 def solution(mesh):
+    def per_device(tokens, *rest):
+        gathered = mesh.size * tokens.size * tokens.dtype.itemsize
+        plan = gather_plan if gathered <= 16 << 20 else dispatch_plan
+        return plan(tokens, *rest)
+
     return jax.shard_map(
         per_device,
         mesh=mesh,

time: 388 us -> 337 us (0.87)
  blocking collectives: 67 us -> 40 us
  waiting for transfers between devices: 204 us -> 185 us
  other arithmetic: 31.4 us -> 12.8 us
  matrix products: 49.6 us -> 64.8 us
  local copies, waits for them, and re-layouts: 15.1 us -> 21.3 us
  starting transfers between devices: 5.95 us -> 0.08 us
    all_to_all x1 -> x0, blocking collectives: 55.3 us -> none  [per_device(): lax.all_to_all(outgoing, 'ep', split_axis=0, concat_axis=0, tiled=True)]
    all_gather x0 -> x2, blocking collectives: none -> 40 us  [the longest x1 32.6 us: gather_plan(): ids = lax.all_gather(expert_ids, 'ep', axis=0)]
    all_to_all x1 -> x0, waiting for transfers between devices: 33 us -> none  [send_back(): return lax.all_to_all(summed, 'ep', split_axis=0, concat_axis=0, tiled=True)]
    reduce_scatter x2, waiting for transfers between devices: 113 us -> 142 us  [the longest x1 72.3 us: gather_plan(): return lax.psum_scatter(total, 'ep', scatter_dimension=0, tiled=True)]
    another operation x3 -> x0, other arithmetic: 18.2 us -> none
    all_gather x2 -> x1, waiting for transfers between devices: 57.4 us -> 41.4 us  [gather_plan(): every = lax.all_gather(tokens, ('ep', 'tp'), axis=0)]
    psum x1 -> x0, blocking collectives: 11.7 us -> none  [per_device(): logits = lax.psum(partial_logits, 'tp')]
    dot_general x7 -> x8, matrix products: 49.6 us -> 58.7 us  [the longest x1 14.6 us: gather_plan(): up = jnp.einsum('jskd,jdf->jskf', x, w_up, preferred_element_type=F32)]
  transfers between devices with their start and end apart: 5 -> 3, of which waited for: 3 -> 3; matrix products, arithmetic and copies ran while one was open for 14% -> 0% of each run, Pallas kernels for 0% -> 0%
where the time goes in v1:
time: 337 us
  waiting for transfers between devices  185 us (55%)
  matrix products  64.8 us (19%)
  blocking collectives  40 us (12%)
  local copies, waits for them, and re-layouts  21.3 us (6%)
  between operations  13.2 us (4%)
  other arithmetic  12.8 us (4%)
    reduce_scatter x1, waiting for transfers between devices, gather_plan(): return lax.psum_scatter(total, 'ep', scatter_dimension=0, tiled=True)  72.3 us
    reduce_scatter x1, waiting for transfers between devices, gather_plan(): total = lax.psum_scatter(total, 'tp', scatter_dimension=2, tiled=True)  70.1 us
    all_gather x1, waiting for transfers between devices, gather_plan(): every = lax.all_gather(tokens, ('ep', 'tp'), axis=0)  41.4 us
    all_gather x1, blocking collectives, gather_plan(): ids = lax.all_gather(expert_ids, 'ep', axis=0)  32.6 us
    dot_general x1, matrix products, gather_plan(): up = jnp.einsum('jskd,jdf->jskf', x, w_up, preferred_element_type=F32)  14.6 us
    dot_general x1, matrix products, gather_plan(): gate = jnp.einsum('jskd,jdf->jskf', x, w_gate, preferred_element_type=F32)  12.8 us
    dot_general x1, matrix products, gather_plan(): routed = jnp.einsum('sjkt,jskd->std', pick, y, preferred_element_type=F32)  12.5 us
    convert_element_type x1, local copies, waits for them, and re-layouts, gather_plan(): values = whole.reshape(n_ep, rows, full).astype(F32)  11.5 us
  transfers between devices with their start and end apart: 3, of which 3 were waited for; matrix products, arithmetic and copies ran while one was open for 0% of the time, Pallas kernels for 0%

profile of v1, /device:TPU:0, one launch (start us, length us, event | category | flops | bytes accessed | tf_op | source)
XLA Modules:
  0.0 336.9 jit_solution(2355705554324601349)
XLA Ops:
  6.5 0.0 all-gather.4.cloned.1.call-start
  6.5 0.7 all-gather.4.cloned.1.call-update
  7.3 0.0 reduce-scatter.3.cloned.1.call-start
  7.3 0.8 reshape.59
  8.1 32.6 %all-gather = s32[2048,4]{0,1:T(4,128)S(1)} all-gather(s32[256,4]{0,1:T(4,128)} %param.15), channel_id=2, replica_groups=mesh['ep'=8,'tp'=4] {'ep'}, dimensions={0}, use_global_device_ids=true | all-gather | bytes 36864 | tf_op jit(solution)/shard_map/all_gather | solution.py:115
  40.7 7.4 %all_gather.19 = bf16[2048,60]{0,1:T(8,128)(2,1)} all-gather(bf16[512,60]{0,1:T(8,128)(2,1)} %param.13), channel_id=1, replica_groups=mesh['ep'=8,'tp'=4] {'tp'}, dimensions={0}, use_global_device_ids=true | all-gather | bytes 307200 | tf_op jit(solution)/shard_map/all_gather | solution.py:116
  48.1 0.1 compare_reduce_fusion
  48.2 0.3 fusion.29
  48.5 41.4 %all-gather.4.cloned.1.call-done = bf16[8192,512]{1,0:T(8,128)(2,1)} async-done(((bf16[256,512]{1,0:T(8,128)(2,1)}), bf16[8192,512]{1,0:T(8,128)(2,1)}) %all-gather.4.cloned.1.call-update) | async-done | bytes 8388624 | tf_op jit(solution)/shard_map/all_gather | solution.py:114
  89.9 11.5 %copy.38 = f32[8,4,32,8,512]{4,3,1,2,0:T(8,128)} copy(bf16[8,4,32,8,512]{4,3,2,1,0:T(8,128)(2,1)} %bitcast.78) | data formatting | bytes 25165824 | tf_op jit(solution)/shard_map/convert_element_type | solution.py:119
  101.5 5.1 %multiply_reduce_fusion = f32[8192]{0:T(1024)S(1)} fusion(bf16[8192,512]{1,0:T(8,128)(2,1)} %all-gather.4.cloned.1.call-done), kind=kLoop, calls=%fused_computation.3 | loop fusion | flops 12574720 | bytes 8421376 | tf_op jit(solution)/shard_map/reduce_sum | solution.py:120
  106.7 0.0 copy-done.3
  106.7 0.0 copy-start.4
  106.7 7.1 %multiply_convert_fusion.1 = bf16[8,256,2048]{2,1,0:T(8,128)(2,1)S(1)} fusion(f32[8,256,2048]{2,1,0:T(8,128)} %bitcast.77, f32[2048]{0:T(1024)S(1)} %copy-done.3, f32[8,256]{1,0:T(8,128)S(1)} %add_rsqrt_fusion), kind=kLoop, calls=%fused_computation.5 | loop fusion | flops 12582912 | bytes 25182208 | tf_op jit(solution)/shard_map/convert_element_type | solution.py:121
  113.8 0.0 copy-done.4
  113.8 0.0 copy-start.2
  113.8 2.3 fusion.31
  116.1 1.1 copy-done.2
  117.3 0.4 fusion.33
  117.6 6.1 %fusion.51 = f32[8,256,60]{1,2,0:T(8,128)S(1)} fusion(bf16[8,256,2048]{2,1,0:T(8,128)(2,1)} %copy-done.2, bf16[2048,60]{0,1:T(8,128)(2,1)} %all_gather.19), kind=kOutput, calls=%fused_computation.51 | convolution fusion | flops 503566464 | bytes 9125888 | tf_op jit(solution)/shard_map/div | solution.py:124
  123.8 8.9 %convert_bitcast_fusion = bf16[8,8,32,2048]{3,2,0,1:T(8,128)(2,1)} fusion(bf16[8,256,2048]{2,1,0:T(8,128)(2,1)} %copy-done.2, s32[8,8,256]{2,1,0:T(8,128)S(1)} %fusion.29), kind=kOutput, calls=%fused_computation.17 | convolution fusion | flops 2152202240 | bytes 16842752 | tf_op jit(solution)/shard_map/sjkt,std->jskd/dot_general | solution.py:137
  132.7 0.4 select_reduce_fusion
  133.2 12.8 %fusion.4 = f32[8,8,32,352]{3,2,1,0:T(8,128)} fusion(bf16[8,2048,352]{1,2,0:T(8,128)(2,1)} %param.16, bf16[8,8,32,2048]{3,2,0,1:T(8,128)(2,1)} %convert_bitcast_fusion), kind=kOutput, calls=%fused_computation.8 | convolution fusion | flops 2952790016 | bytes 22806528 | tf_op jit(solution)/shard_map/jskd,jdf->jskf/dot_general | solution.py:138
  146.0 14.6 %multiply_convert_fusion.3 = bf16[8,8,32,352]{3,2,1,0:T(8,128)(2,1)} fusion(f32[8,8,32,352]{3,2,1,0:T(8,128)} %fusion.4, bf16[8,2048,352]{1,2,0:T(8,128)(2,1)} %param.17, bf16[8,8,32,2048]{3,2,0,1:T(8,128)(2,1)} %convert_bitcast_fusion), kind=kOutput, calls=%fused_computation.20 | convolution fusion | flops 2957115392 | bytes 24248320 | tf_op jit(solution)/shard_map/jskd,jdf->jskf/dot_general | solution.py:139
  160.5 7.0 %convolution_multiply_fusion = f32[256,2048]{1,0:T(8,128)} fusion(bf16[704,2048]{1,0:T(8,128)(2,1)S(1)} %copy-done, f32[256]{0:T(256)S(1)} %add_divide_fusion, bf16[2048,704]{0,1:T(8,128)(2,1)} %param.20, bf16[8,256,2048]{2,1,0:T(8,128)(2,1)} %copy-done.2, s32[]{:T(128)S(6)} %select_n.27, f32[256,704]{0,1:T(8,128)} %fusion.31), kind=kOutput, calls=%fused_computation.21 | convolution fusion | flops 1478000640 | bytes 9634820 | tf_op jit(solution)/shard_map/dot_general | solution.py:149
  167.5 12.5 %fusion.1 = bf16[8,256,2048]{2,1,0:T(8,128)(2,1)} fusion(f32[256,2048]{1,0:T(8,128)} %convolution_multiply_fusion, pred[8]{0:T(512)(128)(4,1)S(1)} %iota_compare_fusion.4, f32[8,8,32]{2,0,1:T(8,128)S(1)} %bitcast.82, bf16[8,352,2048]{2,1,0:T(8,128)(2,1)} %param.18, bf16[8,8,32,352]{3,2,1,0:T(8,128)(2,1)} %multiply_convert_fusion.3, s32[8,8,256]{2,1,0:T(8,128)S(1)} %fusion.29), kind=kOutput, calls=%fused_computation.2 | convolution fusion | flops 5121769472 | bytes 23535624 | tf_op jit(solution)/shard_map/sjkt,jskd->std/dot_general | solution.py:143
  180.0 7.9 %copy.49 = bf16[8,32,4,8,512]{4,3,1,0,2:T(8,128)(2,1)} copy(bf16[8,32,4,8,512]{4,3,2,1,0:T(8,128)(2,1)} %bitcast.76) | data formatting | bytes 16777216 | tf_op jit(solution)/shard_map/reshape | solution.py:154
  187.8 0.0 reduce-scatter.3.cloned.1.call-update
  187.9 0.0 reduce-scatter.5.cloned.1.call-start
  187.9 70.1 %reduce-scatter.3.cloned.1.call-done = bf16[8,256,1,512]{3,1,0,2:T(8,128)(2,1)} async-done(((bf16[8,256,4,512]{3,1,0,2:T(8,128)(2,1)}), bf16[8,256,1,512]{3,1,0,2:T(8,128)(2,1)}) %reduce-scatter.3.cloned.1.call-update) | async-done | bytes 2097168 | tf_op jit(solution)/shard_map/reduce_scatter | solution.py:155
  258.0 0.0 reduce-scatter.5.cloned.1.call-update
  258.1 72.3 %reduce-scatter.5.cloned.1.call-done = bf16[256,512]{1,0:T(8,128)(2,1)} async-done(((bf16[2048,512]{1,0:T(8,128)(2,1)}), bf16[256,512]{1,0:T(8,128)(2,1)}) %reduce-scatter.5.cloned.1.call-update) | async-done | bytes 262160 | tf_op jit(solution)/shard_map/reduce_scatter | solution.py:157
  (13 shorter events, 0.1 us)
Async XLA Ops:
  6.5 154.0 %copy-start = (bf16[704,2048]{1,0:T(8,128)(2,1)S(1)}, bf16[704,2048]{1,0:T(8,128)(2,1)}, u32[]{:S(2)}) copy-start(bf16[704,2048]{1,0:T(8,128)(2,1)} %param.21) | copy-start | bytes 8650756
  6.5 83.4 %all-gather.4.cloned.1.call-start = ((), (), s32[]{:S(2)}) async-start(), calls=%async_computation.4 | async-start | bytes 8650752 | tf_op jit(solution)/shard_map/all_gather | solution.py:114
  7.3 250.8 %reduce-scatter.3.cloned.1.call-start = ((), (), s32[]{:S(2)}) async-start(), calls=%async_computation.2 | async-start | bytes 10485760 | tf_op jit(solution)/shard_map/reduce_scatter | solution.py:155
  101.5 5.2 %copy-start.3 = (f32[2048]{0:T(1024)S(1)}, f32[2048]{0:T(1024)}, u32[]{:S(2)}) copy-start(f32[2048]{0:T(1024)} %param.12) | copy-start | bytes 24580
  106.7 7.1 %copy-start.4 = (bf16[2048,704]{0,1:T(8,128)(2,1)S(1)}, bf16[2048,704]{0,1:T(8,128)(2,1)}, u32[]{:S(2)}) copy-start(bf16[2048,704]{0,1:T(8,128)(2,1)} %param.19) | copy-start | bytes 8650756
  113.8 3.4 %copy-start.2 = (bf16[8,256,2048]{2,1,0:T(8,128)(2,1)}, bf16[8,256,2048]{2,1,0:T(8,128)(2,1)S(1)}, u32[]{:S(2)}) copy-start(bf16[8,256,2048]{2,1,0:T(8,128)(2,1)S(1)} %multiply_convert_fusion.1) | copy-start | bytes 25165828
  180.0 150.4 %copy-start.1 = (bf16[704,2048]{1,0:T(8,128)(2,1)S(1)}, bf16[704,2048]{1,0:T(8,128)(2,1)}, u32[]{:S(2)}) copy-start(bf16[704,2048]{1,0:T(8,128)(2,1)} %param.21) | copy-start | bytes 8650756
  187.9 142.5 %reduce-scatter.5.cloned.1.call-start = ((), (), s32[]{:S(2)}) async-start(), calls=%async_computation.3 | async-start | bytes 2359296 | tf_op jit(solution)/shard_map/reduce_scatter | solution.py:157
Sparse Core Ops, SparseCore 0:
  10.2 79.7 all-gather.3
  188.0 70.0 reduce-scatter.2
  261.6 68.7 reduce-scatter.4
